TPU v7x, 512 devices: a whole 4x4x16 slice. The times are simulated.
512 devices in a mesh: freq: 16 (over y, z_hi, core), stn: 32 (over x, z_lo).
Axes of the slice: x: 4, y: 4, z: 16 (z_hi: 2, z_lo: 8; z = z_hi * 8 + z_lo), core: 2. Of those that a mesh axis runs over, the one named last changes fastest.
Arguments:
- samples: bfloat16 [16, 1024, 24, 2, 128], P('freq', 'stn'), may hold values from -8 to 8, as said below
- window: float32 [128], replicated, may hold values from 0.1 to 1
- group_of_device: int32 [32], replicated, may hold values from 0 to 31, each once
- owner_map: int32 [32, 32], replicated, may hold values from 0 to 31, as said below
Outputs:
- owned: bfloat16 [2, 128, 32, 32, 1024], P(None, None, 'stn', 'freq')
Inputs may be any that keep to these rules, and one draw needn't show every extreme that they name: `samples`: samples are finite and bounded. Every row and every column of owner_map names each stn index exactly once.
All inputs are finite; a program needn't handle non-finite values.
Results may differ from a plain program's by a relative error of at most 0.0065.
Values may be sent and summed in bfloat16 or wider, within the bound.
A program may use at most 64 MiB of HBM per device.

v0:
```python
import math

import jax
import jax.numpy as jnp
from jax import lax
from jax.sharding import PartitionSpec as P

FFT_LEN = 128
AVG = 16
SPEC = 24
CH_OUT = 8


def channel_matrix(window):
    length = window.shape[0]
    index = jnp.arange(length, dtype=jnp.int32)
    product = index[:, None] * index[None, :] % length
    theta = product.astype(jnp.float32) * (2.0 * math.pi / length)
    weights = window[:, None] / math.sqrt(length)
    cosine = weights * jnp.cos(theta)
    sine = weights * jnp.sin(theta)
    upper = jnp.concatenate([cosine, -sine], axis=1)
    lower = jnp.concatenate([sine, cosine], axis=1)
    return jnp.concatenate([upper, lower], axis=0)


def split_matrix(matrix):
    high = matrix.astype(jnp.bfloat16)
    low = (matrix - high.astype(jnp.float32)).astype(jnp.bfloat16)
    return (high, low)


def channelize(block, high, low):
    rows = block.shape[0]
    flat = block.reshape(rows * SPEC, 2 * FFT_LEN)
    spectra = jnp.dot(flat, high, preferred_element_type=jnp.float32) + jnp.dot(
        flat, low, preferred_element_type=jnp.float32
    )
    spectra = spectra.astype(jnp.bfloat16).reshape(rows, SPEC, 2, CH_OUT, AVG)
    return spectra.transpose(3, 0, 2, 1, 4).reshape(CH_OUT, rows, 2 * SPEC * AVG)


def with_swapped(spectra):
    half = spectra.shape[2] // 2
    return jnp.stack(
        [spectra, jnp.concatenate([spectra[..., half:], -spectra[..., :half]], axis=-1)]
    )


def correlate(stacked, remote):
    block = jnp.einsum("pcak,cbk->pcab", stacked, remote, preferred_element_type=jnp.float32)
    return (block * (1.0 / (AVG * SPEC))).astype(jnp.bfloat16)


def channel_plan(local, group_of_device, owner_map, device_of_group, here, groups):
    rows_in = local.shape[1]
    spread = groups // CH_OUT
    quarter = here % spread
    copies = jnp.repeat(local, spread, axis=0)
    turned = lax.all_to_all(copies, "stn", split_axis=0, concat_axis=1, tiled=True)
    span = CH_OUT * rows_in
    mine = lax.dynamic_slice_in_dim(turned, quarter * span, span, 1)
    block = correlate(with_swapped(mine), turned)
    order = jnp.arange(groups, dtype=jnp.int32)
    column_for = (
        jnp.zeros((groups, groups), jnp.int32)
        .at[order[:, None], owner_map]
        .set(jnp.broadcast_to(order[None, :], (groups, groups)))
    )
    row_source = quarter * CH_OUT + jnp.arange(CH_OUT, dtype=jnp.int32)
    row_group = group_of_device[row_source]
    column_device = device_of_group[column_for[row_group]]
    vis = block.reshape(2, CH_OUT, rows_in, groups, rows_in).transpose(0, 1, 3, 2, 4)
    picked = jnp.take_along_axis(vis, column_device[None, :, :, None, None], axis=2)
    outgoing = picked.reshape(2, CH_OUT, groups, rows_in * rows_in)
    received = lax.all_to_all(outgoing, "stn", split_axis=2, concat_axis=2, tiled=True)
    arranged = received.reshape(2, CH_OUT, CH_OUT, spread, rows_in * rows_in).transpose(
        0, 2, 3, 1, 4
    )
    arranged = arranged.reshape(2, CH_OUT, groups, rows_in * rows_in)
    return jnp.take(arranged, device_of_group, axis=2)


def shards(samples, window, group_of_device, owner_map):
    groups = lax.axis_size("stn")
    here = lax.axis_index("stn")
    high, low = split_matrix(channel_matrix(window))
    local = channelize(samples[0], high, low)
    order = jnp.arange(groups, dtype=jnp.int32)
    device_of_group = jnp.zeros((groups,), jnp.int32).at[group_of_device].set(order)
    by_group = channel_plan(local, group_of_device, owner_map, device_of_group, here, groups)
    regrouped = lax.all_to_all(by_group, "freq", split_axis=2, concat_axis=1, tiled=True)
    return regrouped[:, :, None]


def solution(mesh):
    return jax.shard_map(
        shards,
        mesh=mesh,
        in_specs=(P("freq", "stn", None, None, None), P(), P(), P()),
        out_specs=P(None, None, "stn", "freq", None),
        check_vma=False,
    )
```

profile of v0, /device:TPU:39, one launch (start us, length us, event | category | flops | bytes accessed | tf_op | source)
XLA Modules:
  0.0 259.2 jit_solution(11298759052951287189)
XLA Ops:
  0.0 0.7 broadcast_multiply_fusion
  0.7 0.3 fusion.19
  0.9 1.3 fusion.6
  2.3 1.3 fusion.2
  3.6 3.4 %reshape.112 = bf16[32,24,2,8,16]{1,0,4,3,2:T(8,128)(2,1)S(1)} reshape(bf16[768,256]{0,1:T(8,128)(2,1)S(1)} %fusion.2) | data formatting | bytes 786432 | tf_op jit(solution)/shard_map/reshape | solution.py:39
  7.0 2.9 %copy.21 = bf16[8,32,2,24,16]{1,4,3,2,0:T(8,128)(2,1)} copy(bf16[8,32,2,24,16]{3,1,4,0,2:T(8,128)(2,1)S(1)} %bitcast.71) | data formatting | bytes 786432 | tf_op jit(solution)/shard_map/transpose | solution.py:40
  9.9 1.6 copy.22
  11.5 0.0 copy-start.1
  11.5 1.3 broadcast_in_dim.55
  12.9 0.0 copy-start.2
  12.9 0.0 copy-start
  12.9 14.8 %all-to-all-start = ((bf16[32,32,768]{2,1,0:T(8,128)(2,1)}), bf16[32,32,768]{2,1,0:T(8,128)(2,1)S(1)}, u32[]{:S(2)}, u32[]{:S(2)}) async-start(bf16[32,32,768]{2,1,0:T(8,128)(2,1)} %bitcast.8), calls=%async_computation | async-start | bytes 3145728 | tf_op jit(solution)/shard_map/all_to_all | solution.py:60
  27.7 0.0 copy-done.1
  27.7 0.0 copy-done.2
  27.8 0.1 multiply_reduce_fusion
  27.8 0.1 reshape.170
  27.9 0.1 reshape.172
  28.0 4.3 %scatter_custom_fusion.1 = s32[1024]{0:T(1024)S(1)} fusion(s32[1024]{0:T(1024)S(1)} %reshape.170, s32[1024]{0:T(1024)S(1)} %reshape.172, s32[]{:T(128)} %constant.35.clone.1), kind=kCustom, calls=%fused_computation.63 | custom fusion | bytes 4100
  32.3 0.1 reshape.123
  32.4 0.0 copy-done
  32.4 0.6 gather_fusion
  33.1 0.6 gather_fusion.1
  33.6 0.1 reshape.142
  33.7 0.7 scatter_custom_fusion
  34.4 1.9 gather_fusion.2
  36.3 0.1 gather.30
  36.4 0.1 reshape.141
  36.5 0.1 reshape.156
  36.5 62.7 %all-to-all-done = bf16[32,32,768]{2,1,0:T(8,128)(2,1)S(1)} async-done(((bf16[32,32,768]{2,1,0:T(8,128)(2,1)}), bf16[32,32,768]{2,1,0:T(8,128)(2,1)S(1)}, u32[]{:S(2)}, u32[]{:S(2)}) %all-to-all-start) | async-done | bytes 1572896 | tf_op jit(solution)/shard_map/all_to_all | solution.py:60
  99.3 0.1 maximum_bitcast_fusion.2
  99.4 1.0 fusion
  100.4 3.4 %reshape.117 = bf16[2,8,32,32,32]{2,1,4,3,0:T(8,128)(2,1)} reshape(bf16[2,1,256,1024]{2,3,0,1:T(8,128)(2,1)S(1)} %fusion) | data formatting | bytes 2097152 | tf_op jit(solution)/shard_map/reshape | solution.py:73
  103.8 6.7 %copy.23 = bf16[2,8,32,32,32]{4,2,3,1,0:T(8,128)(2,1)} copy(bf16[2,8,32,32,32]{2,1,4,3,0:T(8,128)(2,1)} %reshape.117) | data formatting | bytes 2097152 | tf_op jit(solution)/shard_map/reshape | solution.py:73
  110.5 5.5 %gather_fusion.4 = bf16[256,2,32,32]{3,2,1,0:T(8,128)(2,1)} fusion(bf16[2,8,32,32,32]{4,3,2,1,0:T(8,128)(2,1)} %bitcast.69, s32[256]{0:T(256)S(1)} %reshape.156), kind=kCustom, calls=%fused_computation.4 | custom fusion | bytes 2099200 | tf_op jit(solution)/shard_map/jit(take_along_axis)/gather | solution.py:74
  116.1 5.2 %copy.43 = bf16[8,32,2,32,32]{4,3,1,0,2:T(8,128)(2,1)} copy(bf16[8,32,2,32,32]{4,3,2,1,0:T(8,128)(2,1)} %bitcast.70) | data formatting | bytes 2097152 | tf_op jit(solution)/shard_map/jit(take_along_axis)/gather | solution.py:74
  121.3 6.2 %gather.32 = bf16[2,8,32,1024]{3,2,1,0:T(8,128)(2,1)S(1)} reshape(bf16[2,8,32,32,32]{4,3,2,1,0:T(8,128)(2,1)} %bitcast.68) | data formatting | bytes 2097152 | tf_op jit(solution)/shard_map/jit(take_along_axis)/gather | solution.py:74
  127.5 0.2 broadcast_select_fusion
  127.6 1.5 copy.25
  129.2 7.7 %all-to-all-start.1 = ((bf16[2,8,32,1024]{3,1,0,2:T(8,128)(2,1)}), bf16[2,8,32,1024]{3,1,0,2:T(8,128)(2,1)S(1)}, u32[]{:S(2)}, u32[]{:S(2)}) async-start(bf16[2,8,32,1024]{3,1,0,2:T(8,128)(2,1)} %copy.25), calls=%async_computation.1 | async-start | bytes 2097152 | tf_op jit(solution)/shard_map/all_to_all | solution.py:76
  136.9 49.3 %all-to-all-done.1 = bf16[2,8,32,1024]{3,1,0,2:T(8,128)(2,1)S(1)} async-done(((bf16[2,8,32,1024]{3,1,0,2:T(8,128)(2,1)}), bf16[2,8,32,1024]{3,1,0,2:T(8,128)(2,1)S(1)}, u32[]{:S(2)}, u32[]{:S(2)}) %all-to-all-start.1) | async-done | bytes 1048608 | tf_op jit(solution)/shard_map/all_to_all | solution.py:76
  186.2 0.1 copy.26
  186.3 0.6 copy.27
  186.9 0.6 gather_fusion.3
  187.5 0.2 select_bitcast_fusion
  187.7 69.4 %all_to_all.32 = bf16[2,8,32,1024]{3,1,0,2:T(8,128)(2,1)S(1)} all-to-all(bf16[2,8,32,1024]{3,1,0,2:T(8,128)(2,1)S(1)} %select_bitcast_fusion), channel_id=1, replica_groups=mesh['freq'=16,'stn'=32] {'freq'}, dimensions={2} | all-to-all | bytes 2097152 | tf_op jit(solution)/shard_map/all_to_all | solution.py:92
  257.0 0.1 copy.44
  257.1 2.0 copy.30
  (19 shorter events, 0.2 us)
Async XLA Ops:
  11.5 16.2 %copy-start.1 = (s32[32,32]{1,0:T(8,128)S(1)}, s32[32,32]{1,0:T(8,128)}, u32[]{:S(2)}) copy-start(s32[32,32]{1,0:T(8,128)} %param.7) | copy-start | bytes 12292
  12.9 14.9 %copy-start.2 = (s32[2]{0:T(128)S(1)}, s32[2]{0:T(128)}, u32[]{:S(2)}) copy-start(s32[2]{0:T(128)} %constant.84) | copy-start | bytes 28
  12.9 19.5 %copy-start = (s32[32]{0:T(128)S(1)}, s32[32]{0:T(128)}, u32[]{:S(2)}) copy-start(s32[32]{0:T(128)} %param.6) | copy-start | bytes 388
  12.9 86.4 %all-to-all-start = ((bf16[32,32,768]{2,1,0:T(8,128)(2,1)}), bf16[32,32,768]{2,1,0:T(8,128)(2,1)S(1)}, u32[]{:S(2)}, u32[]{:S(2)}) async-start(bf16[32,32,768]{2,1,0:T(8,128)(2,1)} %bitcast.8), calls=%async_computation | async-start | bytes 3145728 | tf_op jit(solution)/shard_map/all_to_all | solution.py:60
  129.2 57.0 %all-to-all-start.1 = ((bf16[2,8,32,1024]{3,1,0,2:T(8,128)(2,1)}), bf16[2,8,32,1024]{3,1,0,2:T(8,128)(2,1)S(1)}, u32[]{:S(2)}, u32[]{:S(2)}) async-start(bf16[2,8,32,1024]{3,1,0,2:T(8,128)(2,1)} %copy.25), calls=%async_computation.1 | async-start | bytes 2097152 | tf_op jit(solution)/shard_map/all_to_all | solution.py:76
where the time goes:
time: 260 us; the launch traced here: 259 us
  waiting for transfers between devices  112 us (43%)
  blocking collectives  69.4 us (27%)
  local copies, waits for them, and re-layouts  49.8 us (19%)
  starting transfers between devices  22.5 us (9%)
  matrix products  3.63 us (1%)
    all_to_all x1, blocking collectives, shards(): lax.all_to_all(by_group, 'freq', split_axis=2, concat_axis=1, tiled=True)  69.4 us
    all_to_all x1, waiting for transfers between devices, channel_plan(): lax.all_to_all(copies, 'stn', split_axis=0, concat_axis=1, tiled=True)  62.7 us
    all_to_all x1, waiting for transfers between devices, channel_plan(): lax.all_to_all(outgoing, 'stn', split_axis=2, concat_axis=2, tiled=True)  49.3 us
    gather x4, local copies, waits for them, and re-layouts, channel_plan(): jnp.take_along_axis(vis, column_device[None, :, :, None, None], axis=2)  17 us
    all_to_all x1, starting transfers between devices, channel_plan(): lax.all_to_all(copies, 'stn', split_axis=0, concat_axis=1, tiled=True)  14.8 us
    reshape x2, local copies, waits for them, and re-layouts, channel_plan(): block.reshape(2, CH_OUT, rows_in, groups, rows_in).transpose(0, 1, 3, 2, 4)  10.1 us
    all_to_all x1, starting transfers between devices, channel_plan(): lax.all_to_all(outgoing, 'stn', split_axis=2, concat_axis=2, tiled=True)  7.67 us
  transfers between devices with their start and end apart: 2, of which 2 were waited for; matrix products, arithmetic and copies ran while one was open for 3% of the time, Pallas kernels for 0%

commit v1 on v0

v1 whole, which is shorter than its diff:
```python
import math

import jax
import jax.numpy as jnp
import numpy as np
from jax import lax
from jax.experimental import pallas as pl
from jax.experimental.pallas import tpu as pltpu
from jax.sharding import PartitionSpec as P

FFT_LEN = 128
AVG = 16
SPEC = 24
CH_OUT = 8
ROWS = 32
DEPTH = 2 * SPEC * AVG
NX = 4
NZ = 8
NF = 16
STN = NX * NZ
MESH = pl.DeviceIdType.MESH


def dft_table():
    index = np.arange(FFT_LEN)
    theta = (index[:, None] * index[None, :] % FFT_LEN) * (2.0 * math.pi / FFT_LEN)
    table = np.concatenate([np.cos(theta), np.sin(theta)], axis=1) / math.sqrt(FFT_LEN)
    return table.astype(np.float32)


def swap_blocks(blocks, width, lane):
    blocks = list(blocks)
    step = 1
    while step < len(blocks):
        low = (lane // (width * step)) % 2 == 0
        shift = width * step
        for i in range(len(blocks)):
            if i & step:
                continue
            a, b = blocks[i], blocks[i | step]
            blocks[i] = jnp.where(low, a, pltpu.roll(b, shift, 1))
            blocks[i | step] = jnp.where(low, pltpu.roll(a, 128 - shift, 1), b)
        step *= 2
    return blocks


def kernel(
    rows_tab, cols_tab, samples, taps, out,
    uc, us, chan, held, mixed, pairs, outgoing,
    in_send, in_recv, out_send, out_recv, own_sem,
):
    f = lax.axis_index("freq")
    s = lax.axis_index("stn")
    x = s // NZ
    zl = s % NZ

    high = taps[...].astype(jnp.bfloat16)
    low = (taps[...] - high.astype(jnp.float32)).astype(jnp.bfloat16)
    both = jnp.concatenate([high, low], axis=0)
    chunk = 256

    @pl.loop(0, 2 * ROWS * SPEC // chunk)
    def _(i):
        rows = pl.ds(pl.multiple_of(i * chunk, chunk), chunk)
        block = samples[rows, :]
        full = jnp.dot(
            jnp.concatenate([block, block], axis=1), both, preferred_element_type=jnp.float32
        )
        uc[rows, :] = full[:, :FFT_LEN]
        us[rows, :] = full[:, FFT_LEN:]

    lane = lax.broadcasted_iota(jnp.int32, (ROWS, 128), 1)
    for t8 in range(SPEC // 8):
        for part in range(2):
            blocks = []
            for t in range(8):
                at = 2 * (t8 * 8 + t)
                re = pl.ds(at, ROWS, stride=2 * SPEC)
                im = pl.ds(at + 1, ROWS, stride=2 * SPEC)
                if part == 0:
                    blocks.append(uc[re, :] + us[im, :])
                else:
                    blocks.append(uc[im, :] - us[re, :])
            blocks = swap_blocks(blocks, AVG, lane)
            for k in range(CH_OUT):
                start = (2 * t8 + part) * 128
                chan[k, :, start : start + 128] = blocks[k].astype(jnp.bfloat16)
    held[s] = chan[zl]

    def block_to(src, at, to_x, to_z):
        return pltpu.make_async_remote_copy(
            src_ref=src,
            dst_ref=held.at[at],
            send_sem=in_send,
            recv_sem=in_recv.at[at],
            device_id=(f, to_x * NZ + to_z),
            device_id_type=MESH,
        )

    def along_x(src, at):
        for dx in (1, 3, 2):
            block_to(src, at, (x + dx) % NX, zl).start()

    steps = (1, 7, 2, 6, 3, 5, 4)
    for dz in steps:
        to = (zl + dz) % NZ
        block_to(chan.at[to], s, x, to).start()
    along_x(chan.at[zl], s)
    for dz in steps:
        at = x * NZ + (zl - dz + NZ) % NZ
        block_to(held.at[at], at, (x + 1) % NX, zl).wait_recv()
        along_x(held.at[at], at)
    for dx in (1, 3, 2):
        for z in range(NZ):
            at = ((x + dx) % NX) * NZ + z
            block_to(held.at[at], at, (x + 1) % NX, zl).wait_recv()

    lane8 = lax.broadcasted_iota(jnp.int32, (8, 128), 1)
    channel = f * CH_OUT + zl

    @pl.loop(0, NF)
    def _(i):
        p = (f + i) % NF
        for r in range(2):
            g1 = 2 * p + r
            a = held[rows_tab[g1]]
            turned = []
            for t8 in range(SPEC // 8):
                turned.append(a[:, (2 * t8 + 1) * 128 : (2 * t8 + 2) * 128])
                turned.append(-a[:, 2 * t8 * 128 : (2 * t8 + 1) * 128])
            left = jnp.concatenate([a, jnp.concatenate(turned, axis=1)], axis=0)
            right = jnp.concatenate(
                [held[cols_tab[g1, x * NZ + oz]] for oz in range(NZ)], axis=0
            )
            vis = lax.dot_general(
                left, right, (((1,), (1,)), ((), ())), preferred_element_type=jnp.float32
            ) * (1.0 / (AVG * SPEC))
            for h in range(2):
                mixed[r, h] = vis[:, h * 128 : (h + 1) * 128]
                for part in range(2):
                    blocks = [
                        mixed[r, h, pl.ds(part * ROWS + j, 8, stride=4), :] for j in range(4)
                    ]
                    blocks = swap_blocks(blocks, ROWS, lane8)
                    for q in range(4):
                        pairs[4 * h + q, part, pl.ds(r, 8, stride=2), :] = blocks[q]
        outgoing[i] = pairs[...].astype(jnp.bfloat16)
        for oz in range(NZ):
            mine = jnp.logical_and(i == 0, zl == oz)

            @pl.when(jnp.logical_not(mine))
            def _():
                pltpu.make_async_remote_copy(
                    src_ref=outgoing.at[i, oz],
                    dst_ref=out.at[:, channel],
                    send_sem=out_send,
                    recv_sem=out_recv,
                    device_id=(p, x * NZ + oz),
                    device_id_type=MESH,
                ).start()

            @pl.when(mine)
            def _():
                pltpu.make_async_copy(
                    outgoing.at[0, oz], out.at[:, channel], own_sem
                ).start()

    pltpu.make_async_copy(outgoing.at[0, 0], out.at[:, channel], own_sem).wait()
    rest = pltpu.make_async_remote_copy(
        src_ref=out.at[:, pl.ds(0, NF * NZ - 1)],
        dst_ref=out.at[:, pl.ds(0, NF * NZ - 1)],
        send_sem=out_send,
        recv_sem=out_recv,
        device_id=(f, x * NZ + (zl + 1) % NZ),
        device_id_type=MESH,
    )
    rest.wait_send()
    rest.wait_recv()
    sent = pltpu.make_async_remote_copy(
        src_ref=held.at[pl.ds(0, STN - 1)],
        dst_ref=held.at[pl.ds(0, STN - 1)],
        send_sem=in_send,
        recv_sem=in_recv.at[0],
        device_id=(f, x * NZ + (zl + 1) % NZ),
        device_id_type=MESH,
    )
    sent.wait_send()


def shards(samples, window, group_of_device, owner_map):
    order = jnp.arange(STN, dtype=jnp.int32)
    at_group = group_of_device[None, :] == order[:, None]
    rows_tab = jnp.sum(jnp.where(at_group, order[None, :], 0), axis=1)
    hit = owner_map[:, :, None] == order[None, None, :]
    cols_tab = jnp.sum(jnp.where(hit, rows_tab[None, :, None], 0), axis=1)
    taps = window[:, None] * jnp.asarray(dft_table())
    flat = samples.reshape(2 * ROWS * SPEC, FFT_LEN)
    smem = pl.BlockSpec(memory_space=pltpu.SMEM)
    vmem = pl.BlockSpec(memory_space=pltpu.VMEM)
    got = pl.pallas_call(
        kernel,
        out_shape=jax.ShapeDtypeStruct((2, NF * CH_OUT, 16, 128), jnp.bfloat16),
        in_specs=[smem, smem, vmem, vmem],
        out_specs=pl.BlockSpec(memory_space=pl.ANY),
        scratch_shapes=[
            pltpu.VMEM((2 * ROWS * SPEC, FFT_LEN), jnp.float32),
            pltpu.VMEM((2 * ROWS * SPEC, FFT_LEN), jnp.float32),
            pltpu.VMEM((CH_OUT, ROWS, DEPTH), jnp.bfloat16),
            pltpu.VMEM((STN, ROWS, DEPTH), jnp.bfloat16),
            pltpu.VMEM((2, 2, 2 * ROWS, 128), jnp.float32),
            pltpu.VMEM((NZ, 2, 16, 128), jnp.float32),
            pltpu.VMEM((NF, NZ, 2, 16, 128), jnp.bfloat16),
            pltpu.SemaphoreType.DMA,
            pltpu.SemaphoreType.DMA((STN,)),
            pltpu.SemaphoreType.DMA,
            pltpu.SemaphoreType.DMA,
            pltpu.SemaphoreType.DMA,
        ],
        compiler_params=pltpu.CompilerParams(
            has_side_effects=True, vmem_limit_bytes=32 * 1024 * 1024
        ),
        name="correlate_and_regroup",
    )(rows_tab, cols_tab, flat, taps)
    got = got.reshape(2, NF * CH_OUT, 8, 2, 128).transpose(0, 1, 3, 2, 4)
    return got.reshape(2, NF * CH_OUT, 1, 2, ROWS * ROWS)


def solution(mesh):
    return jax.shard_map(
        shards,
        mesh=mesh,
        in_specs=(P("freq", "stn", None, None, None), P(), P(), P()),
        out_specs=P(None, None, "stn", "freq", None),
        check_vma=False,
    )
```

time: 260 us -> 110 us (0.42)
  the two profiles are of different devices: /device:TPU:39 before, /device:TPU:1 now
where the time goes in v1:
time: 110 us
  Pallas kernels  105 us (95%)
  local copies, waits for them, and re-layouts  2.62 us (2%)
  other arithmetic  2.08 us (2%)
    pallas_call x1, Pallas kernels, shards(): pl.pallas_call(kernel, out_shape=jax.ShapeDtypeStruct((2, NF * CH_OUT, 16...  105 us
    unnamed x7, local copies, waits for them, and re-layouts  2.62 us

profile of v1, /device:TPU:1, one launch (start us, length us, event | category | flops | bytes accessed | tf_op | source)
XLA Modules:
  0.0 109.7 jit_solution(6565833414787502822)
XLA Ops:
  0.0 0.0 copy-start.2
  0.0 0.7 copy-done.2
  0.7 0.1 select_reduce_fusion.1.rows_tab
  0.8 0.0 copy-start.1
  0.8 1.0 select_reduce_fusion.cols_tab
  1.8 0.0 copy-done.1
  1.8 1.0 broadcast_multiply_fusion.taps
  2.8 0.0 copy-start
  2.8 1.0 copy-done
  3.8 105.0 %correlate_and_regroup.1 = bf16[2,128,16,128]{3,2,1,0:T(8,128)(2,1)S(1)} custom-call(s32[32]{0:T(128)S(1)} %select_reduce_fusion.1.rows_tab, s32[32,32]{1,0:T(8,128)S(1)} %select_reduce_fusion.cols_tab, bf16[1536,128]{1,0:T(8,128)(2,1)S(1)} %bitcast.7, f32[128,256]{1,0:T(8,128)S(1)} %broadcast_multiply_fusion.taps), custom_call_target="tpu_custom_call" | custom-call | tf_op jit(solution)/shard_map/correlate_and_regroup/pallas_call | solution.py:200
  108.8 1.0 copy.9
Async XLA Ops:
  0.0 0.7 copy-start.2
  0.8 1.0 copy-start.1
  2.8 1.0 copy-start

commit v2 on v1

--- a/solution.py
+++ b/solution.py
@@ -53,6 +53,18 @@
     s = lax.axis_index("stn")
     x = s // NZ
     zl = s % NZ
+
+    barrier = pltpu.get_barrier_semaphore()
+
+    def greet(to_f, to_s):
+        pl.semaphore_signal(barrier, inc=1, device_id=(to_f, to_s), device_id_type=MESH)
+
+    for d in range(1, NZ):
+        greet(f, x * NZ + (zl + d) % NZ)
+    for d in range(1, NX):
+        greet(f, ((x + d) % NX) * NZ + zl)
+    for d in range(1, NF):
+        greet((f + d) % NF, s)
 
     high = taps[...].astype(jnp.bfloat16)
     low = (taps[...] - high.astype(jnp.float32)).astype(jnp.bfloat16)
@@ -86,6 +98,7 @@
                 start = (2 * t8 + part) * 128
                 chan[k, :, start : start + 128] = blocks[k].astype(jnp.bfloat16)
     held[s] = chan[zl]
+    pl.semaphore_wait(barrier, NZ + NX + NF - 3)
 
     def block_to(src, at, to_x, to_z):
         return pltpu.make_async_remote_copy(
@@ -217,7 +230,7 @@
             pltpu.SemaphoreType.DMA,
         ],
         compiler_params=pltpu.CompilerParams(
-            has_side_effects=True, vmem_limit_bytes=32 * 1024 * 1024
+            has_side_effects=True, collective_id=0, vmem_limit_bytes=32 * 1024 * 1024
         ),
         name="correlate_and_regroup",
     )(rows_tab, cols_tab, flat, taps)

time: 110 us -> 95.9 us (0.87)
  Pallas kernels: 105 us -> 90.9 us
    pallas_call x1, Pallas kernels: 105 us -> 90.9 us  [shards(): pl.pallas_call(kernel, out_shape=jax.ShapeDtypeStruct((2, NF * CH_OUT, 16...]
where the time goes in v2:
time: 95.9 us; the launch traced here: 95.7 us
  Pallas kernels  90.9 us (95%)
  local copies, waits for them, and re-layouts  2.62 us (3%)
  other arithmetic  2.08 us (2%)
    pallas_call x1, Pallas kernels, shards(): pl.pallas_call(kernel, out_shape=jax.ShapeDtypeStruct((2, NF * CH_OUT, 16...  90.9 us
    unnamed x7, local copies, waits for them, and re-layouts  2.62 us

profile of v2, /device:TPU:1, one launch (start us, length us, event | category | flops | bytes accessed | tf_op | source)
XLA Modules:
  0.0 95.7 jit_solution(18217237489571380797)
XLA Ops:
  0.0 0.0 copy-start.2
  0.0 0.7 copy-done.2
  0.7 0.1 select_reduce_fusion.1.rows_tab
  0.8 0.0 copy-start.1
  0.8 1.0 %select_reduce_fusion.cols_tab = s32[32,32]{1,0:T(8,128)S(1)} fusion(s32[32]{0:T(128)S(1)} %select_reduce_fusion.1.rows_tab, s32[32,32]{1,0:T(8,128)} %param.8), kind=kLoop, calls=%fused_computation | loop fusion | flops 97280 | bytes 8320 | tf_op jit(solution)/shard_map/reduce_sum | solution.py:208
  1.8 0.0 copy-done.1
  1.8 1.0 %broadcast_multiply_fusion.taps = f32[128,256]{1,0:T(8,128)S(1)} fusion(f32[128,256]{1,0:T(8,128)} %constant.4.clone, f32[128]{0:T(128)S(1)} %copy-done.1), kind=kLoop, calls=%fused_computation.2 | loop fusion | flops 32768 | bytes 262656 | tf_op jit(solution)/shard_map/mul | solution.py:209
  2.8 0.0 copy-start
  2.8 1.0 %copy-done = bf16[1,32,24,2,128]{4,3,2,1,0:T(2,128)(2,1)S(1)} copy-done((bf16[1,32,24,2,128]{4,3,2,1,0:T(2,128)(2,1)S(1)}, bf16[1,32,24,2,128]{4,3,2,1,0:T(2,128)(2,1)}, u32[]{:S(2)}) %copy-start) | copy-done | bytes 393240
  3.8 90.9 %correlate_and_regroup.1 = bf16[2,128,16,128]{3,2,1,0:T(8,128)(2,1)S(1)} custom-call(s32[32]{0:T(128)S(1)} %select_reduce_fusion.1.rows_tab, s32[32,32]{1,0:T(8,128)S(1)} %select_reduce_fusion.cols_tab, bf16[1536,128]{1,0:T(8,128)(2,1)S(1)} %bitcast.7, f32[128,256]{1,0:T(8,128)S(1)} %broadcast_multiply_fusion.taps), custom_call_target="tpu_custom_call" | custom-call | tf_op jit(solution)/shard_map/correlate_and_regroup/pallas_call | solution.py:213
  94.7 1.0 %copy.9 = bf16[2,128,1,2,1024]{4,3,2,1,0:T(2,128)(2,1)} copy(bf16[2,128,1,2,1024]{4,3,2,1,0:T(2,128)(2,1)S(1)} %bitcast.6) | data formatting | bytes 2097152
Async XLA Ops:
  0.0 0.7 copy-start.2
  0.8 1.0 %copy-start.1 = (f32[128]{0:T(128)S(1)}, f32[128]{0:T(128)}, u32[]{:S(2)}) copy-start(f32[128]{0:T(128)} %param.6) | copy-start | bytes 1540
  2.8 1.0 %copy-start = (bf16[1,32,24,2,128]{4,3,2,1,0:T(2,128)(2,1)S(1)}, bf16[1,32,24,2,128]{4,3,2,1,0:T(2,128)(2,1)}, u32[]{:S(2)}) copy-start(bf16[1,32,24,2,128]{4,3,2,1,0:T(2,128)(2,1)} %param.5) | copy-start | bytes 1179652

commit v3 on v2

--- a/solution.py
+++ b/solution.py
@@ -44,10 +44,17 @@
     return blocks
 
 
+def column(row, size):
+    lane = lax.broadcasted_iota(jnp.int32, (size, size), 1)
+    sub = lax.broadcasted_iota(jnp.int32, (size, size), 0)
+    return jnp.sum(jnp.where(lane == sub, row, jnp.zeros_like(row)), axis=1, keepdims=True)
+
+
 def kernel(
-    rows_tab, cols_tab, samples, taps, out,
+    samples_hbm, window_hbm, groups_hbm, owners_hbm, table_hbm, out,
+    samples, window, groups, owners, table, tab_vmem, tab,
     uc, us, chan, held, mixed, pairs, outgoing,
-    in_send, in_recv, out_send, out_recv, own_sem,
+    load_sem, chunk_sem, in_send, in_recv, out_send, out_recv, own_sem,
 ):
     f = lax.axis_index("freq")
     s = lax.axis_index("stn")
@@ -66,14 +73,39 @@
     for d in range(1, NF):
         greet((f + d) % NF, s)
 
-    high = taps[...].astype(jnp.bfloat16)
-    low = (taps[...] - high.astype(jnp.float32)).astype(jnp.bfloat16)
+    loads = [
+        pltpu.make_async_copy(src, dst, load_sem.at[n])
+        for n, (src, dst) in enumerate(
+            [(window_hbm, window), (table_hbm, table), (groups_hbm, groups), (owners_hbm, owners)]
+        )
+    ]
+    chunk = 256
+    chunks = 2 * ROWS * SPEC // chunk
+
+    def load_chunk(i):
+        rows = pl.ds(pl.multiple_of(i * chunk, chunk), chunk)
+        return pltpu.make_async_copy(
+            samples_hbm.at[rows, :], samples.at[rows, :], chunk_sem.at[i]
+        )
+
+    loads[0].start()
+    loads[1].start()
+    for i in range(chunks):
+        load_chunk(i).start()
+    loads[2].start()
+    loads[3].start()
+
+    loads[0].wait()
+    loads[1].wait()
+    taps = table[...] * column(window[...], FFT_LEN)
+    high = taps.astype(jnp.bfloat16)
+    low = (taps - high.astype(jnp.float32)).astype(jnp.bfloat16)
     both = jnp.concatenate([high, low], axis=0)
-    chunk = 256
-
-    @pl.loop(0, 2 * ROWS * SPEC // chunk)
+
+    @pl.loop(0, chunks)
     def _(i):
         rows = pl.ds(pl.multiple_of(i * chunk, chunk), chunk)
+        load_chunk(i).wait()
         block = samples[rows, :]
         full = jnp.dot(
             jnp.concatenate([block, block], axis=1), both, preferred_element_type=jnp.float32
@@ -119,6 +151,26 @@
         to = (zl + dz) % NZ
         block_to(chan.at[to], s, x, to).start()
     along_x(chan.at[zl], s)
+
+    loads[2].wait()
+    loads[3].wait()
+    wide = lax.broadcasted_iota(jnp.int32, (STN, STN), 1)
+    tall = lax.broadcasted_iota(jnp.int32, (STN, STN), 0)
+    group_row = groups[...]
+    row_source = jnp.max(jnp.where(group_row == tall, wide, 0), axis=1, keepdims=True)
+    source_row = jnp.max(
+        jnp.where(column(group_row, STN) == wide, tall, 0), axis=0, keepdims=True
+    )
+    place = lax.broadcasted_iota(jnp.int32, (STN, 128), 1)
+    sources = jnp.where(place == NZ, row_source, 0)
+    for oz in range(NZ):
+        picked = jnp.where(owners[...] == x * NZ + oz, source_row, 0)
+        sources = jnp.where(place == oz, jnp.max(picked, axis=1, keepdims=True), sources)
+    tab_vmem[...] = sources
+    to_scalars = pltpu.make_async_copy(tab_vmem, tab, load_sem.at[0])
+    to_scalars.start()
+    to_scalars.wait()
+
     for dz in steps:
         at = x * NZ + (zl - dz + NZ) % NZ
         block_to(held.at[at], at, (x + 1) % NX, zl).wait_recv()
@@ -136,14 +188,14 @@
         p = (f + i) % NF
         for r in range(2):
             g1 = 2 * p + r
-            a = held[rows_tab[g1]]
+            a = held[tab[g1, NZ]]
             turned = []
             for t8 in range(SPEC // 8):
                 turned.append(a[:, (2 * t8 + 1) * 128 : (2 * t8 + 2) * 128])
                 turned.append(-a[:, 2 * t8 * 128 : (2 * t8 + 1) * 128])
             left = jnp.concatenate([a, jnp.concatenate(turned, axis=1)], axis=0)
             right = jnp.concatenate(
-                [held[cols_tab[g1, x * NZ + oz]] for oz in range(NZ)], axis=0
+                [held[tab[g1, oz]] for oz in range(NZ)], axis=0
             )
             vis = lax.dot_general(
                 left, right, (((1,), (1,)), ((), ())), preferred_element_type=jnp.float32
@@ -201,21 +253,21 @@
 
 
 def shards(samples, window, group_of_device, owner_map):
-    order = jnp.arange(STN, dtype=jnp.int32)
-    at_group = group_of_device[None, :] == order[:, None]
-    rows_tab = jnp.sum(jnp.where(at_group, order[None, :], 0), axis=1)
-    hit = owner_map[:, :, None] == order[None, None, :]
-    cols_tab = jnp.sum(jnp.where(hit, rows_tab[None, :, None], 0), axis=1)
-    taps = window[:, None] * jnp.asarray(dft_table())
     flat = samples.reshape(2 * ROWS * SPEC, FFT_LEN)
-    smem = pl.BlockSpec(memory_space=pltpu.SMEM)
-    vmem = pl.BlockSpec(memory_space=pltpu.VMEM)
+    hbm = pl.BlockSpec(memory_space=pltpu.HBM)
     got = pl.pallas_call(
         kernel,
         out_shape=jax.ShapeDtypeStruct((2, NF * CH_OUT, 16, 128), jnp.bfloat16),
-        in_specs=[smem, smem, vmem, vmem],
+        in_specs=[hbm] * 5,
         out_specs=pl.BlockSpec(memory_space=pl.ANY),
         scratch_shapes=[
+            pltpu.VMEM((2 * ROWS * SPEC, FFT_LEN), jnp.bfloat16),
+            pltpu.VMEM((1, FFT_LEN), jnp.float32),
+            pltpu.VMEM((1, STN), jnp.int32),
+            pltpu.VMEM((STN, STN), jnp.int32),
+            pltpu.VMEM((FFT_LEN, 2 * FFT_LEN), jnp.float32),
+            pltpu.VMEM((STN, 128), jnp.int32),
+            pltpu.SMEM((STN, 128), jnp.int32),
             pltpu.VMEM((2 * ROWS * SPEC, FFT_LEN), jnp.float32),
             pltpu.VMEM((2 * ROWS * SPEC, FFT_LEN), jnp.float32),
             pltpu.VMEM((CH_OUT, ROWS, DEPTH), jnp.bfloat16),
@@ -223,6 +275,8 @@
             pltpu.VMEM((2, 2, 2 * ROWS, 128), jnp.float32),
             pltpu.VMEM((NZ, 2, 16, 128), jnp.float32),
             pltpu.VMEM((NF, NZ, 2, 16, 128), jnp.bfloat16),
+            pltpu.SemaphoreType.DMA((4,)),
+            pltpu.SemaphoreType.DMA((6,)),
             pltpu.SemaphoreType.DMA,
             pltpu.SemaphoreType.DMA((STN,)),
             pltpu.SemaphoreType.DMA,
@@ -230,10 +284,16 @@
             pltpu.SemaphoreType.DMA,
         ],
         compiler_params=pltpu.CompilerParams(
-            has_side_effects=True, collective_id=0, vmem_limit_bytes=32 * 1024 * 1024
+            has_side_effects=True, collective_id=0, vmem_limit_bytes=62 * 1024 * 1024
         ),
         name="correlate_and_regroup",
-    )(rows_tab, cols_tab, flat, taps)
+    )(
+        flat,
+        window.reshape(1, FFT_LEN),
+        group_of_device.reshape(1, STN),
+        owner_map,
+        jnp.asarray(dft_table()),
+    )
     got = got.reshape(2, NF * CH_OUT, 8, 2, 128).transpose(0, 1, 3, 2, 4)
     return got.reshape(2, NF * CH_OUT, 1, 2, ROWS * ROWS)
 

time: 95.9 us -> 93.7 us (0.977)
  other arithmetic: 2.08 us -> 0 us
    reduce_sum x2 -> x0, other arithmetic: 1.09 us -> none  [the longest x1 0.98 us: shards(): cols_tab = jnp.sum(jnp.where(hit, rows_tab[None, :, None], 0), axis=1)]
    mul x1 -> x0, other arithmetic: 0.99 us -> none  [shards(): taps = window[:, None] * jnp.asarray(dft_table())]
    unnamed x7 -> x1, local copies, waits for them, and re-layouts: 2.62 us -> 2.91 us
where the time goes in v3:
time: 93.7 us; the launch traced here: 93.5 us
  Pallas kernels  90.6 us (97%)
  local copies, waits for them, and re-layouts  2.91 us (3%)
    pallas_call x1, Pallas kernels, shards(): pl.pallas_call(kernel, out_shape=jax.ShapeDtypeStruct((2, NF * CH_OUT, 16...  90.6 us
    unnamed x1, local copies, waits for them, and re-layouts  2.91 us

profile of v3, /device:TPU:1, one launch (start us, length us, event | category | flops | bytes accessed | tf_op | source)
XLA Modules:
  0.0 93.5 jit_solution(13394621909943414976)
XLA Ops:
  0.0 90.6 %correlate_and_regroup.1 = bf16[2,128,16,128]{3,2,1,0:T(8,128)(2,1)} custom-call(bf16[1536,128]{1,0:T(8,128)(2,1)} %bitcast.9, f32[1,128]{1,0:T(1,128)} %bitcast.10, s32[1,32]{1,0:T(1,128)} %bitcast.11, s32[32,32]{1,0:T(8,128)} %owners_hbm.1, f32[128,256]{1,0:T(8,128)} %constant.2.clone.table_hbm), custom_call_target="tpu_custom_call" | custom-call | tf_op jit(solution)/shard_map/correlate_and_regroup/pallas_call | solution.py:258
  90.6 2.9 %copy.8 = bf16[2,128,1,2,1024]{4,3,2,1,0:T(2,128)(2,1)} copy(bf16[2,128,1,2,1024]{4,3,2,1,0:T(2,128)(2,1)} %bitcast.8) | data formatting | bytes 2097152

commit v4 on v3

--- a/solution.py
+++ b/solution.py
@@ -19,6 +19,7 @@
 NF = 16
 STN = NX * NZ
 MESH = pl.DeviceIdType.MESH
+PLAN = ((0, 1), (0, 2), (0, 3), (1, 0), (1, 1), (1, 2), (1, 3))
 
 
 def dft_table():
@@ -54,7 +55,7 @@
     samples_hbm, window_hbm, groups_hbm, owners_hbm, table_hbm, out,
     samples, window, groups, owners, table, tab_vmem, tab,
     uc, us, chan, held, mixed, pairs, outgoing,
-    load_sem, chunk_sem, in_send, in_recv, out_send, out_recv, own_sem,
+    load_sem, chunk_sem, in_send, in_recv, out_send, out_recv, own_sem, heard, crossed, known,
 ):
     f = lax.axis_index("freq")
     s = lax.axis_index("stn")
@@ -62,16 +63,24 @@
     zl = s % NZ
 
     barrier = pltpu.get_barrier_semaphore()
-
-    def greet(to_f, to_s):
-        pl.semaphore_signal(barrier, inc=1, device_id=(to_f, to_s), device_id_type=MESH)
+    flip = f + 2 - 4 * ((f // 2) % 2)
+    facing = x * NZ + NZ - 1 - zl
+    border = jnp.logical_or(zl == 0, zl == NZ - 1)
+
+    def signal(semaphore, to_f, to_s):
+        pl.semaphore_signal(semaphore, inc=1, device_id=(to_f, to_s), device_id_type=MESH)
 
     for d in range(1, NZ):
-        greet(f, x * NZ + (zl + d) % NZ)
+        signal(barrier, f, x * NZ + (zl + d) % NZ)
     for d in range(1, NX):
-        greet(f, ((x + d) % NX) * NZ + zl)
-    for d in range(1, NF):
-        greet((f + d) % NF, s)
+        signal(barrier, f, ((x + d) % NX) * NZ + zl)
+    for d in range(1, NF // 2):
+        y_core = (f // 4 * 2 + f % 2 + d) % (NF // 2)
+        signal(barrier, y_core // 2 * 4 + f // 2 % 2 * 2 + y_core % 2, s)
+
+    @pl.when(border)
+    def _():
+        signal(barrier, flip, facing)
 
     loads = [
         pltpu.make_async_copy(src, dst, load_sem.at[n])
@@ -130,7 +139,25 @@
                 start = (2 * t8 + part) * 128
                 chan[k, :, start : start + 128] = blocks[k].astype(jnp.bfloat16)
     held[s] = chan[zl]
-    pl.semaphore_wait(barrier, NZ + NX + NF - 3)
+
+    @pl.when(border)
+    def _():
+        pl.semaphore_wait(barrier, NZ + NX + NF // 2 - 2)
+
+    @pl.when(jnp.logical_not(border))
+    def _():
+        pl.semaphore_wait(barrier, NZ + NX + NF // 2 - 3)
+
+    @pl.when(zl != NZ - 1)
+    def _():
+        signal(heard, f, x * NZ + NZ - 1)
+
+
+    half = NZ // 2
+
+    def turn(n, way):
+        other, step = PLAN[n]
+        return (zl // half + other) % 2 * half + (zl + half + way * step) % half
 
     def block_to(src, at, to_x, to_z):
         return pltpu.make_async_remote_copy(
@@ -142,15 +169,17 @@
             device_id_type=MESH,
         )
 
-    def along_x(src, at):
-        for dx in (1, 3, 2):
-            block_to(src, at, (x + dx) % NX, zl).start()
-
-    steps = (1, 7, 2, 6, 3, 5, 4)
-    for dz in steps:
-        to = (zl + dz) % NZ
+    def share(at):
+        for dx in (2, 1, 3):
+            block_to(held.at[at], at, (x + dx) % NX, zl).start()
+
+    def arrived(at):
+        block_to(held.at[at], at, (x + 1) % NX, zl).wait_recv()
+
+    for n in range(NZ - 1):
+        to = turn(n, 1)
         block_to(chan.at[to], s, x, to).start()
-    along_x(chan.at[zl], s)
+    share(s)
 
     loads[2].wait()
     loads[3].wait()
@@ -171,14 +200,32 @@
     to_scalars.start()
     to_scalars.wait()
 
-    for dz in steps:
-        at = x * NZ + (zl - dz + NZ) % NZ
-        block_to(held.at[at], at, (x + 1) % NX, zl).wait_recv()
-        along_x(held.at[at], at)
-    for dx in (1, 3, 2):
+    for n in range(NZ - 1):
+        at = x * NZ + turn(n, -1)
+        arrived(at)
+        share(at)
+        if n == 3:
+
+            @pl.when(zl == NZ - 1)
+            def _():
+                pl.semaphore_wait(heard, NZ - 1)
+                signal(crossed, flip, facing)
+
+        if n == 5:
+
+            @pl.when(zl == 0)
+            def _():
+                pl.semaphore_wait(crossed, 1)
+                for z in range(1, NZ):
+                    signal(known, f, x * NZ + z)
+
+    for dx in range(1, NX):
         for z in range(NZ):
-            at = ((x + dx) % NX) * NZ + z
-            block_to(held.at[at], at, (x + 1) % NX, zl).wait_recv()
+            arrived((x + dx) % NX * NZ + z)
+
+    @pl.when(zl != 0)
+    def _():
+        pl.semaphore_wait(known, 1)
 
     lane8 = lax.broadcasted_iota(jnp.int32, (8, 128), 1)
     channel = f * CH_OUT + zl
@@ -282,17 +329,25 @@
             pltpu.SemaphoreType.DMA,
             pltpu.SemaphoreType.DMA,
             pltpu.SemaphoreType.DMA,
+            pltpu.SemaphoreType.REGULAR,
+            pltpu.SemaphoreType.REGULAR,
+            pltpu.SemaphoreType.REGULAR,
         ],
         compiler_params=pltpu.CompilerParams(
-            has_side_effects=True, collective_id=0, vmem_limit_bytes=62 * 1024 * 1024
+            has_side_effects=True, collective_id=0, vmem_limit_bytes=32 * 1024 * 1024
         ),
         name="correlate_and_regroup",
     )(
-        flat,
-        window.reshape(1, FFT_LEN),
-        group_of_device.reshape(1, STN),
-        owner_map,
-        jnp.asarray(dft_table()),
+        *(
+            pltpu.with_memory_space_constraint(operand, pltpu.HBM)
+            for operand in (
+                flat,
+                window.reshape(1, FFT_LEN),
+                group_of_device.reshape(1, STN),
+                owner_map,
+                jnp.asarray(dft_table()),
+            )
+        )
     )
     got = got.reshape(2, NF * CH_OUT, 8, 2, 128).transpose(0, 1, 3, 2, 4)
     return got.reshape(2, NF * CH_OUT, 1, 2, ROWS * ROWS)

time: 93.7 us -> 88.1 us (0.940)
  Pallas kernels: 90.6 us -> 87 us
  local copies, waits for them, and re-layouts: 2.91 us -> 0.97 us
    pallas_call x1, Pallas kernels: 90.6 us -> 87 us  [shards(): pl.pallas_call(kernel, out_shape=jax.ShapeDtypeStruct((2, NF * CH_OUT, 16...]
    unnamed x1, local copies, waits for them, and re-layouts: 2.91 us -> 0.97 us
where the time goes in v4:
time: 88.1 us; the launch traced here: 88 us
  Pallas kernels  87 us (99%)
  local copies, waits for them, and re-layouts  0.97 us (1%)
    pallas_call x1, Pallas kernels, shards(): pl.pallas_call(kernel, out_shape=jax.ShapeDtypeStruct((2, NF * CH_OUT, 16...  87 us

profile of v4, /device:TPU:1, one launch (start us, length us, event | category | flops | bytes accessed | tf_op | source)
XLA Modules:
  0.0 88.0 jit_solution(2235803106739346591)
XLA Ops:
  0.0 87.0 %correlate_and_regroup.1 = bf16[2,128,16,128]{3,2,1,0:T(8,128)(2,1)S(1)} custom-call(bf16[1536,128]{1,0:T(8,128)(2,1)} %bitcast.9, f32[1,128]{1,0:T(1,128)} %bitcast.10, s32[1,32]{1,0:T(1,128)} %bitcast.11, s32[32,32]{1,0:T(8,128)} %owners_hbm.1, f32[128,256]{1,0:T(8,128)} %constant.2.clone.table_hbm), custom_call_target="tpu_custom_call" | custom-call | tf_op jit(solution)/shard_map/correlate_and_regroup/pallas_call | solution.py:305
  87.0 1.0 %copy.8 = bf16[2,128,1,2,1024]{4,3,2,1,0:T(2,128)(2,1)} copy(bf16[2,128,1,2,1024]{4,3,2,1,0:T(2,128)(2,1)S(1)} %bitcast.8) | data formatting | bytes 2097152

commit v5 on v4

--- a/solution.py
+++ b/solution.py
@@ -20,6 +20,7 @@
 STN = NX * NZ
 MESH = pl.DeviceIdType.MESH
 PLAN = ((0, 1), (0, 2), (0, 3), (1, 0), (1, 1), (1, 2), (1, 3))
+RELAYED = 0
 
 
 def dft_table():
@@ -55,7 +56,7 @@
     samples_hbm, window_hbm, groups_hbm, owners_hbm, table_hbm, out,
     samples, window, groups, owners, table, tab_vmem, tab,
     uc, us, chan, held, mixed, pairs, outgoing,
-    load_sem, chunk_sem, in_send, in_recv, out_send, out_recv, own_sem, heard, crossed, known,
+    load_sem, chunk_sem, in_send, in_recv, out_send, out_recv, own_sem, heard, crossed, known, go,
 ):
     f = lax.axis_index("freq")
     s = lax.axis_index("stn")
@@ -155,9 +156,11 @@
 
     half = NZ // 2
 
-    def turn(n, way):
+    def turn(n):
         other, step = PLAN[n]
-        return (zl // half + other) % 2 * half + (zl + half + way * step) % half
+        high = (zl // 2 + step // 2) % 2
+        low = (zl + step) % 2
+        return (zl // half + other) % 2 * half + high * 2 + low
 
     def block_to(src, at, to_x, to_z):
         return pltpu.make_async_remote_copy(
@@ -169,17 +172,40 @@
             device_id_type=MESH,
         )
 
-    def share(at):
-        for dx in (2, 1, 3):
-            block_to(held.at[at], at, (x + dx) % NX, zl).start()
+    right = (x + 1) % NX
+    left = (x + 3) % NX
+
+    def forward(at, to_x):
+        block_to(held.at[at], at, to_x, zl).start()
+
+    def place_of(of_x, n):
+        return of_x * NZ + (turn(n) if n >= 0 else zl)
+
+    def share(n):
+        at = place_of(x, n)
+        if n + 1 >= RELAYED:
+            forward(at, (x + 2) % NX)
+        forward(at, right if n % 2 else left)
+        forward(at, left if n % 2 else right)
 
     def arrived(at):
-        block_to(held.at[at], at, (x + 1) % NX, zl).wait_recv()
-
-    for n in range(NZ - 1):
-        to = turn(n, 1)
-        block_to(chan.at[to], s, x, to).start()
-    share(s)
+        block_to(held.at[at], at, right, zl).wait_recv()
+
+    def relay(n):
+        came, to_x = (left, right) if n % 2 else (right, left)
+        at = place_of(came, n)
+        arrived(at)
+        forward(at, to_x)
+
+    core = f % 2
+
+    @pl.when(core == 0)
+    def _():
+        for n in range(NZ - 1):
+            to = turn(n)
+            block_to(chan.at[to], s, x, to).start()
+
+    share(-1)
 
     loads[2].wait()
     loads[3].wait()
@@ -200,10 +226,24 @@
     to_scalars.start()
     to_scalars.wait()
 
+    @pl.when(core == 1)
+    def _():
+        pl.semaphore_wait(go, 1)
+        for n in range(NZ - 1):
+            to = turn(n)
+            block_to(chan.at[to], s, x, to).start()
+
     for n in range(NZ - 1):
-        at = x * NZ + turn(n, -1)
-        arrived(at)
-        share(at)
+        arrived(place_of(x, n))
+        share(n)
+        if n - 2 >= -1 and n - 1 < RELAYED:
+            relay(n - 2)
+        if n == 6:
+
+            @pl.when(core == 0)
+            def _():
+                signal(go, f + 1, s)
+
         if n == 3:
 
             @pl.when(zl == NZ - 1)
@@ -219,9 +259,13 @@
                 for z in range(1, NZ):
                     signal(known, f, x * NZ + z)
 
-    for dx in range(1, NX):
-        for z in range(NZ):
-            arrived((x + dx) % NX * NZ + z)
+    for n in range(-1, NZ - 1):
+        if n + 1 < RELAYED:
+            arrived(place_of(right if n % 2 else left, n))
+        else:
+            arrived(place_of(left, n))
+            arrived(place_of(right, n))
+        arrived(place_of((x + 2) % NX, n))
 
     @pl.when(zl != 0)
     def _():
@@ -232,7 +276,8 @@
 
     @pl.loop(0, NF)
     def _(i):
-        p = (f + i) % NF
+        y_core = (f // 4 * 2 + f % 2 + i) % (NF // 2)
+        p = y_core // 2 * 4 + (f // 2 + 1 + i // (NF // 2)) % 2 * 2 + y_core % 2
         for r in range(2):
             g1 = 2 * p + r
             a = held[tab[g1, NZ]]
@@ -257,8 +302,9 @@
                     for q in range(4):
                         pairs[4 * h + q, part, pl.ds(r, 8, stride=2), :] = blocks[q]
         outgoing[i] = pairs[...].astype(jnp.bfloat16)
-        for oz in range(NZ):
-            mine = jnp.logical_and(i == 0, zl == oz)
+        for d in range(NZ):
+            oz = (zl + d) % NZ
+            mine = jnp.logical_and(p == f, d == 0)
 
             @pl.when(jnp.logical_not(mine))
             def _():
@@ -274,7 +320,7 @@
             @pl.when(mine)
             def _():
                 pltpu.make_async_copy(
-                    outgoing.at[0, oz], out.at[:, channel], own_sem
+                    outgoing.at[i, oz], out.at[:, channel], own_sem
                 ).start()
 
     pltpu.make_async_copy(outgoing.at[0, 0], out.at[:, channel], own_sem).wait()
@@ -332,6 +378,7 @@
             pltpu.SemaphoreType.REGULAR,
             pltpu.SemaphoreType.REGULAR,
             pltpu.SemaphoreType.REGULAR,
+            pltpu.SemaphoreType.REGULAR,
         ],
         compiler_params=pltpu.CompilerParams(
             has_side_effects=True, collective_id=0, vmem_limit_bytes=32 * 1024 * 1024

time: 88.1 us -> 82.9 us (0.941); the launches traced: 88 us -> 81.5 us
  Pallas kernels: 87 us -> 80.6 us
    pallas_call x1, Pallas kernels: 87 us -> 80.6 us  [shards(): pl.pallas_call(kernel, out_shape=jax.ShapeDtypeStruct((2, NF * CH_OUT, 16...]
where the time goes in v5:
time: 82.9 us; the launch traced here: 81.5 us
  Pallas kernels  80.6 us (97%)
  local copies, waits for them, and re-layouts  0.97 us (1%)
    pallas_call x1, Pallas kernels, shards(): pl.pallas_call(kernel, out_shape=jax.ShapeDtypeStruct((2, NF * CH_OUT, 16...  80.6 us

profile of v5, /device:TPU:1, one launch (start us, length us, event | category | flops | bytes accessed | tf_op | source)
XLA Modules:
  0.0 81.5 jit_solution(2675404457777963694)
XLA Ops:
  0.0 80.6 %correlate_and_regroup.1 = bf16[2,128,16,128]{3,2,1,0:T(8,128)(2,1)S(1)} custom-call(bf16[1536,128]{1,0:T(8,128)(2,1)} %bitcast.9, f32[1,128]{1,0:T(1,128)} %bitcast.10, s32[1,32]{1,0:T(1,128)} %bitcast.11, s32[32,32]{1,0:T(8,128)} %owners_hbm.1, f32[128,256]{1,0:T(8,128)} %constant.2.clone.table_hbm), custom_call_target="tpu_custom_call" | custom-call | tf_op jit(solution)/shard_map/correlate_and_regroup/pallas_call | solution.py:351
  80.6 1.0 %copy.8 = bf16[2,128,1,2,1024]{4,3,2,1,0:T(2,128)(2,1)} copy(bf16[2,128,1,2,1024]{4,3,2,1,0:T(2,128)(2,1)S(1)} %bitcast.8) | data formatting | bytes 2097152

commit v6 on v5

--- a/solution.py
+++ b/solution.py
@@ -197,9 +197,9 @@
         arrived(at)
         forward(at, to_x)
 
-    core = f % 2
-
-    @pl.when(core == 0)
+    second = 1 - f % 2
+
+    @pl.when(second == 0)
     def _():
         for n in range(NZ - 1):
             to = turn(n)
@@ -226,7 +226,7 @@
     to_scalars.start()
     to_scalars.wait()
 
-    @pl.when(core == 1)
+    @pl.when(second == 1)
     def _():
         pl.semaphore_wait(go, 1)
         for n in range(NZ - 1):
@@ -238,11 +238,11 @@
         share(n)
         if n - 2 >= -1 and n - 1 < RELAYED:
             relay(n - 2)
-        if n == 6:
-
-            @pl.when(core == 0)
+        if n == 5:
+
+            @pl.when(second == 0)
             def _():
-                signal(go, f + 1, s)
+                signal(go, f - 1, s)
 
         if n == 3:
 

time: 82.9 us -> 81.8 us (0.987)
  the two profiles are of different devices: /device:TPU:1 before, /device:TPU:41 now
where the time goes in v6:
time: 81.8 us; the launch traced here: 81.7 us
  Pallas kernels  80.7 us (99%)
  local copies, waits for them, and re-layouts  0.97 us (1%)
    pallas_call x1, Pallas kernels, shards(): pl.pallas_call(kernel, out_shape=jax.ShapeDtypeStruct((2, NF * CH_OUT, 16...  80.7 us

profile of v6, /device:TPU:41, one launch (start us, length us, event | category | flops | bytes accessed | tf_op | source)
XLA Modules:
  0.0 81.7 jit_solution(13776784181151310996)
XLA Ops:
  0.0 80.7 %correlate_and_regroup.1 = bf16[2,128,16,128]{3,2,1,0:T(8,128)(2,1)S(1)} custom-call(bf16[1536,128]{1,0:T(8,128)(2,1)} %bitcast.9, f32[1,128]{1,0:T(1,128)} %bitcast.10, s32[1,32]{1,0:T(1,128)} %bitcast.11, s32[32,32]{1,0:T(8,128)} %owners_hbm.1, f32[128,256]{1,0:T(8,128)} %constant.2.clone.table_hbm), custom_call_target="tpu_custom_call" | custom-call | tf_op jit(solution)/shard_map/correlate_and_regroup/pallas_call | solution.py:351
  80.7 1.0 %copy.8 = bf16[2,128,1,2,1024]{4,3,2,1,0:T(2,128)(2,1)} copy(bf16[2,128,1,2,1024]{4,3,2,1,0:T(2,128)(2,1)S(1)} %bitcast.8) | data formatting | bytes 2097152

commit v7 on v6

--- a/solution.py
+++ b/solution.py
@@ -276,8 +276,8 @@
 
     @pl.loop(0, NF)
     def _(i):
-        y_core = (f // 4 * 2 + f % 2 + i) % (NF // 2)
-        p = y_core // 2 * 4 + (f // 2 + 1 + i // (NF // 2)) % 2 * 2 + y_core % 2
+        y_core = (f // 4 * 2 + f % 2 + jnp.where(second == 0, i // 2, i)) % (NF // 2)
+        p = y_core // 2 * 4 + (f // 2 + 1 + jnp.where(second == 0, i, i // (NF // 2))) % 2 * 2 + y_core % 2
         for r in range(2):
             g1 = 2 * p + r
             a = held[tab[g1, NZ]]

time: 81.8 us -> 81.9 us (level)
  the two profiles are of different devices: /device:TPU:41 before, /device:TPU:1 now
where the time goes in v7:
time: 81.9 us; the launch traced here: 80.6 us
  Pallas kernels  79.6 us (97%)
  local copies, waits for them, and re-layouts  0.97 us (1%)
    pallas_call x1, Pallas kernels, shards(): pl.pallas_call(kernel, out_shape=jax.ShapeDtypeStruct((2, NF * CH_OUT, 16...  79.6 us

profile of v7, /device:TPU:1, one launch (start us, length us, event | category | flops | bytes accessed | tf_op | source)
XLA Modules:
  0.0 80.6 jit_solution(13486095238554889700)
XLA Ops:
  0.0 79.6 %correlate_and_regroup.1 = bf16[2,128,16,128]{3,2,1,0:T(8,128)(2,1)S(1)} custom-call(bf16[1536,128]{1,0:T(8,128)(2,1)} %bitcast.9, f32[1,128]{1,0:T(1,128)} %bitcast.10, s32[1,32]{1,0:T(1,128)} %bitcast.11, s32[32,32]{1,0:T(8,128)} %owners_hbm.1, f32[128,256]{1,0:T(8,128)} %constant.2.clone.table_hbm), custom_call_target="tpu_custom_call" | custom-call | tf_op jit(solution)/shard_map/correlate_and_regroup/pallas_call | solution.py:351
  79.6 1.0 %copy.8 = bf16[2,128,1,2,1024]{4,3,2,1,0:T(2,128)(2,1)} copy(bf16[2,128,1,2,1024]{4,3,2,1,0:T(2,128)(2,1)S(1)} %bitcast.8) | data formatting | bytes 2097152
